TPU v7x, 512 devices: a whole 4x8x8 slice. The times are simulated.
512 devices in a mesh: seq: 64 (over y, z), head: 4 (over x), req: 2 (over core).
Axes of the slice: x: 4, y: 8, z: 8, core: 2. Of those that a mesh axis runs over, the one named last changes fastest.
Arguments:
- queries: bfloat16 [8, 512, 128], P('req', ('head', 'seq')), may hold values from -256 to 256
- key_codes: bfloat16 [8, 8, 32768, 128], P('req', 'head', 'seq'), may hold values from -448 to 448
- key_scale: float32 [8, 8, 512], P('req', 'head', 'seq'), may hold values from 0.01 to 0.1
- value_codes: bfloat16 [8, 8, 32768, 128], P('req', 'head', 'seq'), may hold values from -192 to 192
- value_scale: float32 [8, 8, 512], P('req', 'head', 'seq'), may hold values from 0.01 to 0.06
- out_weight: bfloat16 [16384, 16384], P('head', 'seq'), may hold values from -0.1875 to 0.1875
- ctx_len: int32 [8], P('req'), may hold values from 8192 to 32768, as said below
- start_shard: int32 [8], P('req'), may hold values from 0 to 63
- draft_depth: int32 [8, 4], P('req'), may hold values from 0 to 3
Outputs:
- projected: bfloat16 [4, 8, 16384], P('head', 'req', 'seq')
Inputs may be any that keep to these rules, and one draw needn't show every extreme that they name: `ctx_len`: at least one request has exactly 32768 positions.
All inputs are finite; a program needn't handle non-finite values.
Results may differ from a plain program's by a relative error of at most 0.0057.
Values may be sent and summed in bfloat16 or wider, within the bound.
A program may use at most 64 MiB of HBM per device.

v0:
```python
import math

import jax
import jax.numpy as jnp
from jax import lax
from jax.sharding import Mesh
from jax.sharding import PartitionSpec as P

QHEADS = 128
KVH = 8
HD = 128
DRAFT = 4
BLK = 64
SEQ = ("seq_0", "seq_1")
HEAD_SEQ = ("head", "seq_0", "seq_1")


NEG_FLOOR = -1e30


def copy_for_each(shard, axis):
    copies = jnp.broadcast_to(shard, (lax.axis_size(axis), *shard.shape))
    return lax.all_to_all(copies, axis, split_axis=0, concat_axis=0, tiled=True)


def laid_out(pieces, dim):
    dims = list(pieces.shape[1:])
    dims[dim] *= pieces.shape[0]
    return jnp.moveaxis(pieces, 0, dim).reshape(dims)


def gathered_copies(shard, axis, dim):
    pieces = copy_for_each(shard, axis)
    return laid_out(pieces, dim)


def over_axes(shard, axes):
    for axis in axes:
        shard = lax.pmax(shard, axis)
    return shard


def split_up(shard, dim, size):
    before, after = (shard.shape[:dim], shard.shape[dim + 1 :])
    return jnp.moveaxis(shard.reshape(*before, size, -1, *after), dim, 0)


def sum_at_owner(shard, axis, dim):
    size = lax.axis_size(axis)
    pieces = lax.all_to_all(split_up(shard, dim, size), axis, 0, 0, tiled=True)
    return jnp.sum(pieces, axis=0)


def padded_to(lines, size):
    spare = -len(lines) % size
    return jnp.pad(lines, [(0, spare)] + [(0, 0)] * (lines.ndim - 1))


def nested_sum(shard, axes):
    own = sum_at_owner(padded_to(shard, lax.axis_size(axes)), axes, 0)
    whole = gathered_copies(own, axes, 0)
    return whole[: len(shard)].reshape(shard.shape)


def in_one(arrays, axis):
    ends = [0]
    for a in arrays:
        ends.append(ends[-1] + a.size)
    running = nested_sum(jnp.concatenate([a.ravel() for a in arrays]), axis)
    return tuple((running[b:e].reshape(a.shape) for a, b, e in zip(arrays, ends, ends[1:])))


def shard_partial(block_q, key_block, key_tok, value_block, value_tok, positions, limits):
    raw = jnp.einsum("rhqd,rhkd->rhqk", block_q, key_block, preferred_element_type=jnp.float32)
    scores = raw * (key_tok[:, :, None, :] * (1.0 / math.sqrt(HD)))
    visible = positions[:, None, None, :] <= limits[:, None, :, None]
    masked = jnp.where(visible, scores, NEG_FLOOR)
    top = jnp.max(masked, axis=3)
    weights = jnp.where(visible, jnp.exp(masked - top[..., None]), 0.0)
    total = jnp.sum(weights, axis=3)
    scaled = (weights * value_tok[:, :, None, :]).astype(jnp.bfloat16)
    acc = jnp.einsum("rhqk,rhkd->rhqd", scaled, value_block, preferred_element_type=jnp.float32)
    return (top, total, acc)


def on_device(
    queries,
    key_codes,
    key_scale,
    value_codes,
    value_scale,
    out_weight,
    ctx_len,
    start_shard,
    draft_depth,
):
    seq_count = lax.axis_size(SEQ)
    here = lax.axis_index(SEQ)
    req_dev, rows_dev, head_dim = queries.shape
    kv_heads = key_codes.shape[1]
    kv_rows = key_codes.shape[2]
    group_rows = QHEADS // KVH * DRAFT
    key_tok = jnp.repeat(key_scale, BLK, axis=2)
    value_tok = jnp.repeat(value_scale, BLK, axis=2)
    offsets = jnp.mod(here - start_shard, seq_count)
    positions = offsets[:, None] * kv_rows + jnp.arange(kv_rows, dtype=jnp.int32)[None, :]
    base_limit = ctx_len - DRAFT
    draft_ids = jnp.arange(DRAFT, dtype=jnp.int32)
    whole_q = gathered_copies(queries, SEQ, 1)
    grouped = whole_q.reshape(req_dev, kv_heads, group_rows, head_dim)
    draft_of = jnp.arange(group_rows, dtype=jnp.int32) % DRAFT
    pick = (draft_of[:, None] == draft_ids[None, :]).astype(jnp.int32)
    part = shard_partial(
        grouped,
        key_codes,
        key_tok,
        value_codes,
        value_tok,
        positions,
        base_limit[:, None] + jnp.sum(draft_depth[:, None, :] * pick[None], axis=2),
    )
    top = over_axes(part[0], SEQ)
    rescale = jnp.exp(part[0] - top)
    acc, total = in_one((part[2] * rescale[..., None], part[1] * rescale), SEQ)
    attention = (acc / total[..., None]).astype(jnp.bfloat16)
    gathered = attention.reshape(req_dev, kv_heads * group_rows, head_dim)
    head_count = gathered.shape[1] // DRAFT
    arranged = gathered.reshape(req_dev, head_count, DRAFT, head_dim)
    width_dev = out_weight.shape[1]
    flat = jnp.transpose(arranged, (2, 0, 1, 3)).reshape(
        DRAFT // lax.axis_size("head") * lax.axis_size("head") * req_dev, head_count * head_dim
    )
    result = jnp.dot(flat, out_weight, preferred_element_type=jnp.float32)
    summed = sum_at_owner(
        result.reshape(DRAFT // lax.axis_size("head") * lax.axis_size("head"), req_dev, width_dev),
        "head",
        0,
    )
    return summed.astype(jnp.bfloat16)


def solution(mesh):
    torus = Mesh(
        mesh.devices.reshape(8, 8, mesh.shape["head"], mesh.shape["req"]),
        ("seq_0", "seq_1", "head", "req"),
    )
    placed = (
        P("req", HEAD_SEQ, None),
        P("req", "head", SEQ, None),
        P("req", "head", SEQ),
        P("req", "head", SEQ, None),
        P("req", "head", SEQ),
        P("head", SEQ),
        P("req"),
        P("req"),
        P("req", None),
    )
    return jax.shard_map(
        on_device, mesh=torus, in_specs=placed, out_specs=P("head", "req", SEQ), check_vma=False
    )
```

profile of v0, /device:TPU:2, one launch (start us, length us, event | category | flops | bytes accessed | tf_op | source)
XLA Modules:
  0.0 115.6 jit_solution(3507452771494513746)
XLA Ops:
  0.0 0.0 copy-start
  0.0 1.5 %broadcast_in_dim.42 = bf16[64,4,2,128]{3,2,1,0:T(2,128)(2,1)} broadcast(bf16[4,2,128]{2,1,0:T(2,128)(2,1)} %param.9), dimensions={1,2,3} | broadcast | bytes 133120 | tf_op jit(solution)/shard_map/broadcast_in_dim | solution.py:22
  1.5 16.6 %all-to-all-start = ((bf16[64,4,2,128]{3,2,1,0:T(2,128)(2,1)}), bf16[64,4,2,128]{3,2,1,0:T(2,128)(2,1)S(1)}, u32[]{:S(2)}, u32[]{:S(2)}) async-start(bf16[64,4,2,128]{3,2,1,0:T(2,128)(2,1)} %broadcast_in_dim.42), calls=%async_computation | async-start | bytes 262144 | tf_op jit(solution)/shard_map/all_to_all | solution.py:23
  18.1 0.7 broadcast_multiply_fusion
  18.8 0.7 broadcast_add_fusion.1
  19.5 0.7 fusion.13
  20.2 0.1 iota_add_fusion
  20.2 0.8 multiply_reduce_fusion
  21.0 0.1 broadcast_add_fusion
  21.1 0.1 broadcast_in_dim.43
  21.2 0.1 mul.71
  21.2 0.8 broadcast_in_dim.46
  22.0 0.1 mul.74
  22.1 0.1 broadcast_compare_fusion
  22.2 8.6 %all-to-all-done = bf16[64,4,2,128]{3,2,1,0:T(2,128)(2,1)S(1)} async-done(((bf16[64,4,2,128]{3,2,1,0:T(2,128)(2,1)}), bf16[64,4,2,128]{3,2,1,0:T(2,128)(2,1)S(1)}, u32[]{:S(2)}, u32[]{:S(2)}) %all-to-all-start) | async-done | bytes 131104 | tf_op jit(solution)/shard_map/all_to_all | solution.py:23
  30.8 0.1 copy.17
  30.9 1.8 %fusion.17 = (f32[4,2,64]{2,1,0:T(2,128)S(1)}, f32[4,2,64,512]{3,2,1,0:T(8,128)S(1)}) fusion(f32[4,2,512]{2,1,0:T(2,128)S(1)} %mul.71, bf16[4,2,64,128]{3,2,1,0:T(8,128)(2,1)S(1)} %bitcast.36, bf16[4,2,512,128]{3,2,1,0:T(8,128)(2,1)} %param.10, pred[4,64,512]{2,1,0:T(8,128)(4,1)S(1)} %broadcast_compare_fusion), kind=kOutput, calls=%fused_computation.34 | convolution fusion | flops 67894784 | bytes 2377728 | tf_op jit(solution)/shard_map/rhqd,rhkd->rhqk/dot_general | solution.py:74
  32.7 14.6 %pmax.14 = f32[4,2,64]{2,1,0:T(2,128)S(1)} all-reduce(f32[4,2,64]{2,1,0:T(2,128)S(1)} %get-tuple-element.7), channel_id=1, replica_groups=mesh['seq_0'=8,'seq_1'=8,'head'=4,'req'=2] {'seq_0'}, use_global_device_ids=true, to_apply=%region_2.3 | all-reduce | flops 512 | bytes 4096 | tf_op jit(solution)/shard_map/pmax | solution.py:39
  47.4 0.4 fusion.6
  47.8 15.1 %pmax.15 = f32[4,2,64]{2,1,0:T(2,128)S(1)} all-reduce(f32[4,2,64]{2,1,0:T(2,128)S(1)} %pmax.14), channel_id=1, replica_groups=mesh['seq_0'=8,'seq_1'=8,'head'=4,'req'=2] {'seq_1'}, use_global_device_ids=true, to_apply=%region_3.4 | all-reduce | flops 512 | bytes 4096 | tf_op jit(solution)/shard_map/pmax | solution.py:39
  62.9 0.1 reshape.128
  63.0 1.7 %convolution_multiply_fusion.1 = f32[4,2,64,128]{3,2,1,0:T(8,128)S(1)} fusion(bf16[4,2,512,128]{3,2,1,0:T(8,128)(2,1)} %param.12, f32[4,2,64,512]{3,2,1,0:T(8,128)S(1)} %get-tuple-element.8, f32[4,2,512]{2,1,0:T(2,128)S(1)} %mul.74, f32[4,2,64]{2,1,0:T(2,128)S(1)} %get-tuple-element.7, pred[4,64,512]{2,1,0:T(8,128)(4,1)S(1)} %broadcast_compare_fusion, ...), kind=kOutput, calls=%fused_computation.4 | convolution fusion | flops 68222976 | bytes 2510848 | tf_op jit(solution)/shard_map/rhqk,rhkd->rhqd/dot_general | solution.py:82
  64.7 0.4 all_to_all.17
  65.1 20.9 %all_to_all.25 = f32[64,1,1032]{2,1,0:T(1,128)S(1)} all-to-all(f32[64,1,1032]{2,1,0:T(1,128)S(1)} %all_to_all.17), channel_id=1, replica_groups=mesh['seq_0'=8,'seq_1'=8,'head'=4,'req'=2] {'seq_0','seq_1'}, dimensions={0} | all-to-all | bytes 528384 | tf_op jit(solution)/shard_map/all_to_all | solution.py:50
  86.1 0.2 reduce_sum.38
  86.3 0.2 broadcast_in_dim.47
  86.4 17.7 %all_to_all.26 = f32[64,1,1032]{2,1,0:T(1,128)S(1)} all-to-all(f32[64,1,1032]{2,1,0:T(1,128)S(1)} %broadcast_in_dim.47), channel_id=1, replica_groups=mesh['seq_0'=8,'seq_1'=8,'head'=4,'req'=2] {'seq_0','seq_1'}, dimensions={0} | all-to-all | bytes 528384 | tf_op jit(solution)/shard_map/all_to_all | solution.py:23
  104.1 0.7 reduce.2
  104.8 0.2 reshape.129
  105.0 0.6 slice.10
  105.6 0.1 div.11
  105.7 0.2 fusion.11
  106.0 0.0 copy-done
  106.0 0.4 fusion.3
  106.4 8.5 %all_to_all.27 = f32[4,1,4,256]{3,2,1,0:T(4,128)S(1)} all-to-all(f32[4,1,4,256]{3,2,1,0:T(4,128)S(1)} %fusion.3), channel_id=1, replica_groups=mesh['seq_0'=8,'seq_1'=8,'head'=4,'req'=2] {'head'}, dimensions={0} | all-to-all | bytes 32768 | tf_op jit(solution)/shard_map/all_to_all | solution.py:50
  115.0 0.6 reduce_sum.39
  (8 shorter events, 0.1 us)
Async XLA Ops:
  0.0 106.0 %copy-start = (bf16[4096,256]{1,0:T(8,128)(2,1)S(1)}, bf16[4096,256]{1,0:T(8,128)(2,1)}, u32[]{:S(2)}) copy-start(bf16[4096,256]{1,0:T(8,128)(2,1)} %param.14) | copy-start | bytes 6291460
  1.5 29.3 %all-to-all-start = ((bf16[64,4,2,128]{3,2,1,0:T(2,128)(2,1)}), bf16[64,4,2,128]{3,2,1,0:T(2,128)(2,1)S(1)}, u32[]{:S(2)}, u32[]{:S(2)}) async-start(bf16[64,4,2,128]{3,2,1,0:T(2,128)(2,1)} %broadcast_in_dim.42), calls=%async_computation | async-start | bytes 262144 | tf_op jit(solution)/shard_map/all_to_all | solution.py:23
where the time goes:
time: 116 us
  blocking collectives  76.9 us (66%)
  starting transfers between devices  16.6 us (14%)
  waiting for transfers between devices  8.6 us (7%)
  other arithmetic  5.18 us (4%)
  local copies, waits for them, and re-layouts  4.23 us (4%)
  matrix products  3.88 us (3%)
    pmax x2, blocking collectives, over_axes(): shard = lax.pmax(shard, axis)  29.8 us
    all_to_all x2, blocking collectives, sum_at_owner(): pieces = lax.all_to_all(split_up(shard, dim, size), axis, 0, 0, tiled=True)  29.5 us
    all_to_all x1, blocking collectives, copy_for_each(): return lax.all_to_all(copies, axis, split_axis=0, concat_axis=0, tiled=True)  17.7 us
    all_to_all x1, starting transfers between devices, copy_for_each(): return lax.all_to_all(copies, axis, split_axis=0, concat_axis=0, tiled=True)  16.6 us
    all_to_all x1, waiting for transfers between devices, copy_for_each(): return lax.all_to_all(copies, axis, split_axis=0, concat_axis=0, tiled=True)  8.6 us
  transfers between devices with their start and end apart: 1, of which 1 were waited for; matrix products, arithmetic and copies ran while one was open for 4% of the time, Pallas kernels for 0%

commit v1 on v0

v1 whole, which is shorter than its diff:
```python
import math

import jax
import jax.numpy as jnp
from jax import lax
from jax.experimental import pallas as pl
from jax.experimental.pallas import tpu as pltpu
from jax.sharding import Mesh
from jax.sharding import PartitionSpec as P

QHEADS = 128
KVH = 8
HD = 128
DRAFT = 4
BLK = 64
SEQ = ("seq_0", "seq_1")
HEAD_SEQ = ("head", "seq_0", "seq_1")
MESH = pl.DeviceIdType.MESH

N = 8
NX = 4
R = 4
KV = 2
ROWS = 64
KEYS = 512
NEG = -1e30
FLOOR = -1e29
ORDER = (4, 3, 5, 2, 6, 1, 7)
FIRST = ("seq_1", "seq_0")
SECOND = ("seq_0", "seq_1")


def peer(axis, k, size):
    return lax.rem(lax.axis_index(axis) + k, size)


def f32(x):
    return x.astype(jnp.float32)


def bf16(x):
    return x.astype(jnp.bfloat16)


def kernel(
    q_hbm, k_hbm, ks_hbm, v_hbm, vs_hbm, w_hbm, ctx_hbm, start_hbm, depth_hbm,
    out_ref,
    q0, q1, qf, kbuf, vbuf, wbuf, ks, vs, ctx, start, depth,
    sacc, sst, racc, rst, cacc, cst, dacc, dst, att, ybuf, xbuf,
    lsem, ssem, rsem, xs, xr,
):
    y = lax.axis_index("seq_0")
    z = lax.axis_index("seq_1")
    x = lax.axis_index("head")
    line = {"seq_0": y, "seq_1": z}
    here = y * N + z

    barrier = pltpu.get_barrier_semaphore()
    for axis in SEQ:
        for k in ORDER:
            pl.semaphore_signal(barrier, inc=1, device_id={axis: peer(axis, k, N)}, device_id_type=MESH)
    for k in (2, 1, 3):
        pl.semaphore_signal(barrier, inc=1, device_id={"head": peer("head", k, NX)}, device_id_type=MESH)

    qc0 = pltpu.make_async_copy(q_hbm.at[pl.ds(0, 2)], q0.at[:, z], lsem.at[0])
    qc1 = pltpu.make_async_copy(q_hbm.at[pl.ds(2, 2)], q1.at[:, y], lsem.at[1])
    qc0.start()
    qc1.start()
    small = [
        pltpu.make_async_copy(a, b, lsem.at[2 + i])
        for i, (a, b) in enumerate(
            ((ks_hbm, ks), (vs_hbm, vs), (ctx_hbm, ctx), (start_hbm, start), (depth_hbm, depth))
        )
    ]
    for c in small:
        c.start()
    kc = pltpu.make_async_copy(k_hbm, kbuf, lsem.at[7])
    vc = pltpu.make_async_copy(v_hbm, vbuf, lsem.at[8])
    wc = pltpu.make_async_copy(w_hbm, wbuf, lsem.at[9])
    kc.start()
    vc.start()
    wc.start()
    qc0.wait()
    qc1.wait()
    pl.semaphore_wait(barrier, 2 * (N - 1) + NX - 1)

    sent = []

    def send(src, dst, slot, axis, k):
        copy = pltpu.make_async_remote_copy(
            src_ref=src, dst_ref=dst, send_sem=ssem.at[slot, k - 1], recv_sem=rsem.at[slot, k - 1],
            device_id={axis: peer(axis, k, N)}, device_id_type=MESH,
        )
        copy.start()
        sent.append(copy)

    def arrived(src, dst, slot, axis, k):
        pltpu.make_async_remote_copy(
            src_ref=src, dst_ref=dst, send_sem=ssem.at[slot, k - 1], recv_sem=rsem.at[slot, k - 1],
            device_id={axis: peer(axis, k, N)}, device_id_type=MESH,
        ).wait_recv()

    for k in ORDER:
        send(q0.at[:, z], q0.at[:, z], 0, "seq_1", k)
        send(q1.at[:, y], q1.at[:, y], 1, "seq_0", k)
    for k in ORDER[::-1]:
        zz = peer("seq_1", N - k, N)
        arrived(q0.at[:, z], q0.at[:, zz], 0, "seq_1", k)
    for k in ORDER:
        send(q0, qf.at[pl.ds(0, 2), y], 2, "seq_0", k)
    for k in ORDER[::-1]:
        yy = peer("seq_0", N - k, N)
        arrived(q1.at[:, y], q1.at[:, yy], 1, "seq_0", k)
    for k in ORDER:
        send(q1, qf.at[pl.ds(2, 2), :, z], 3, "seq_1", k)
    qf[0:2, y] = q0[...]
    qf[2:4, :, z] = q1[...]
    for c in small:
        c.wait()

    lane_key = lax.broadcasted_iota(jnp.int32, (ROWS, KEYS), 1)
    lane_row = lax.broadcasted_iota(jnp.int32, (1, HD), 1)
    draft = lax.rem(lax.broadcasted_iota(jnp.int32, (ROWS, 1), 0), DRAFT)
    lane = lax.broadcasted_iota(jnp.int32, (ROWS, HD), 1)
    factor = math.log2(math.e) / math.sqrt(HD)

    def scale_row(ref, r, h, by):
        tiles = []
        for j in range(KEYS // HD):
            tiles.append(jnp.where(lane_row < BLK, ref[r, h, 2 * j] * by, ref[r, h, 2 * j + 1] * by))
        return jnp.concatenate(tiles, axis=1)

    kc.wait()
    vc.wait()
    for half in range(2):
        if half == 0:
            for k in ORDER[::-1]:
                arrived(q0, qf.at[pl.ds(0, 2), peer("seq_0", N - k, N)], 2, "seq_0", k)
        else:
            for k in ORDER[::-1]:
                arrived(q1, qf.at[pl.ds(2, 2), :, peer("seq_1", N - k, N)], 3, "seq_1", k)
        axis = FIRST[half]
        stats = jnp.zeros((ROWS, HD), jnp.float32)
        for r2 in range(2):
            r = half * 2 + r2
            offset = lax.rem(here - start[r] + N * N, N * N) * KEYS
            base = ctx[r] - DRAFT - offset
            limit = jnp.full((ROWS, 1), base + depth[r, 0], jnp.int32)
            for t in range(1, DRAFT):
                limit = jnp.where(draft == t, base + depth[r, t], limit)
            visible = lane_key <= limit
            accs = []
            for h in range(KV):
                rows = qf[r, 4 * h : 4 * h + 4].reshape(ROWS, HD)
                raw = lax.dot_general(
                    rows, kbuf[r, h], (((1,), (1,)), ((), ())), preferred_element_type=jnp.float32
                )
                score = jnp.where(visible, raw * scale_row(ks, r, h, factor), NEG)
                top = jnp.maximum(jnp.max(score, axis=1, keepdims=True), FLOOR)
                weight = jnp.exp2(score - top)
                total = jnp.sum(weight, axis=1, keepdims=True)
                scaled = bf16(weight * scale_row(vs, r, h, 1.0))
                accs.append(jnp.dot(scaled, vbuf[r, h], preferred_element_type=jnp.float32))
                c = r2 * KV + h
                stats = jnp.where(lane == c, top, stats)
                stats = jnp.where(lane == BLK + c, total, stats)
            for o in range(N):
                part = jnp.concatenate([a[8 * o : 8 * o + 8] for a in accs], axis=0)
                sacc[half, o, r2] = bf16(part)
        for o in range(N):
            sst[half, o] = stats[8 * o : 8 * o + 8]
        me = line[axis]
        for k in ORDER:
            to = peer(axis, k, N)
            send(sacc.at[half, to], racc.at[half, me], 4 + half, axis, k)
            send(sst.at[half, to], rst.at[half, me], 6 + half, axis, k)
        racc[half, me] = sacc[half, me]
        rst[half, me] = sst[half, me]

    small_lane = lax.broadcasted_iota(jnp.int32, (8, HD), 1)

    def combine(accs, stats, half, last):
        st = [stats[half, k] for k in range(N)]
        top = st[0]
        for s in st[1:]:
            top = jnp.maximum(top, s)
        fs = [jnp.exp2(s - top) for s in st]
        total = jnp.zeros((8, HD), jnp.float32)
        for s, f in zip(st, fs):
            total = total + pltpu.roll(s, BLK, 1) * f
        if last:
            inv = 1.0 / total
            fs = [f * inv for f in fs]
        outs = []
        for r2 in range(2):
            acc = jnp.zeros((16, HD), jnp.float32)
            for k in range(N):
                w = jnp.concatenate(
                    [jnp.broadcast_to(fs[k][:, r2 * KV + h : r2 * KV + h + 1], (8, HD)) for h in range(KV)],
                    axis=0,
                )
                acc = acc + f32(accs[half, k, r2]) * w
            outs.append(bf16(acc))
        return outs, jnp.where(small_lane < BLK, top, pltpu.roll(total, BLK, 1))

    for half in range(2):
        axis = FIRST[half]
        for k in ORDER[::-1]:
            frm = peer(axis, N - k, N)
            arrived(sacc.at[half, 0], racc.at[half, frm], 4 + half, axis, k)
            arrived(sst.at[half, 0], rst.at[half, frm], 6 + half, axis, k)
        outs, st = combine(racc, rst, half, False)
        for r2 in range(2):
            cacc[half, r2] = outs[r2]
        cst[half] = st
        axis = SECOND[half]
        me = line[axis]
        for k in ORDER:
            send(cacc.at[half], dacc.at[half, me], 8 + half, axis, k)
            send(cst.at[half], dst.at[half, me], 10 + half, axis, k)
        for r2 in range(2):
            dacc[half, me, r2] = outs[r2]
        dst[half, me] = st

    for half in range(2):
        axis = SECOND[half]
        for k in ORDER[::-1]:
            frm = peer(axis, N - k, N)
            arrived(cacc.at[half], dacc.at[half, frm], 8 + half, axis, k)
            arrived(cst.at[half], dst.at[half, frm], 10 + half, axis, k)
        outs, _ = combine(dacc, dst, half, True)
        axis = FIRST[half]
        me = line[axis]
        for r2 in range(2):
            att[me, half, r2] = outs[r2]
        for k in ORDER:
            send(att.at[me, half], att.at[me, half], 12 + half, axis, k)

    wc.wait()
    for half in range(2):
        axis = FIRST[half]
        me = line[axis]
        for k in ORDER[::-1]:
            frm = peer(axis, N - k, N)
            arrived(att.at[me, half], att.at[frm, half], 12 + half, axis, k)

    lhs = jnp.concatenate([att[o].reshape(ROWS, HD) for o in range(N)], axis=1)
    prods = []
    for h in range(KV):
        for jj in range(2):
            w = wbuf[h, :, jj].reshape(N * HD, wbuf.shape[-1])
            prods.append(jnp.dot(lhs, w, preferred_element_type=jnp.float32))
    width = wbuf.shape[-1]
    sub = lax.broadcasted_iota(jnp.int32, (8, width), 0)
    for r in range(R):
        b = r * 16
        first = jnp.where(sub < 4, prods[0][b : b + 8], prods[1][b : b + 8])
        second = jnp.where(sub < 4, prods[2][b + 8 : b + 16], prods[3][b + 8 : b + 16])
        both = first + second
        ybuf[:, r, :] = both[0:4] + both[4:8]

    xcopies = []
    for k in (2, 1, 3):
        to = peer("head", k, NX)
        copy = pltpu.make_async_remote_copy(
            src_ref=ybuf.at[to], dst_ref=xbuf.at[x], send_sem=xs.at[k - 1], recv_sem=xr.at[k - 1],
            device_id={"head": to}, device_id_type=MESH,
        )
        copy.start()
        xcopies.append((k, copy))
    result = ybuf[x]
    for c in sent:
        c.wait_send()
    for k, copy in xcopies:
        frm = peer("head", NX - k, NX)
        pltpu.make_async_remote_copy(
            src_ref=ybuf.at[0], dst_ref=xbuf.at[frm], send_sem=xs.at[k - 1], recv_sem=xr.at[k - 1],
            device_id={"head": frm}, device_id_type=MESH,
        ).wait_recv()
        result = result + xbuf[frm]
    out_ref[0] = bf16(result)
    for k, copy in xcopies:
        copy.wait_send()


def on_device(queries, key_codes, key_scale, value_codes, value_scale, out_weight, ctx_len, start_shard, draft_depth):
    width = out_weight.shape[1]
    weight = out_weight.reshape(KV, N, 2, HD, width)
    dma = pltpu.SemaphoreType.DMA
    b16, flt, i32 = jnp.bfloat16, jnp.float32, jnp.int32
    vm, sm = pltpu.VMEM, pltpu.SMEM
    return pl.pallas_call(
        kernel,
        out_shape=jax.ShapeDtypeStruct((1, R, width), b16),
        in_specs=[pl.BlockSpec(memory_space=pl.ANY)] * 9,
        out_specs=pl.BlockSpec(memory_space=pltpu.VMEM),
        scratch_shapes=[
            vm((2, N, 2, HD), b16),
            vm((2, N, 2, HD), b16),
            vm((R, N, N, 2, HD), b16),
            vm((R, KV, KEYS, HD), b16),
            vm((R, KV, KEYS, HD), b16),
            vm((KV, N, 2, HD, width), b16),
            sm((R, KV, KEYS // BLK), flt),
            sm((R, KV, KEYS // BLK), flt),
            sm((R,), i32),
            sm((R,), i32),
            sm((R, DRAFT), i32),
            vm((2, N, 2, 16, HD), b16),
            vm((2, N, 8, HD), flt),
            vm((2, N, 2, 16, HD), b16),
            vm((2, N, 8, HD), flt),
            vm((2, 2, 16, HD), b16),
            vm((2, 8, HD), flt),
            vm((2, N, 2, 16, HD), b16),
            vm((2, N, 8, HD), flt),
            vm((N, 2, 2, 16, HD), b16),
            vm((DRAFT, R, width), flt),
            vm((NX, R, width), flt),
            dma((10,)),
            dma((14, N - 1)),
            dma((14, N - 1)),
            dma((NX - 1,)),
            dma((NX - 1,)),
        ],
        compiler_params=pltpu.CompilerParams(collective_id=0, has_side_effects=True),
        name="draft_attention",
    )(queries, key_codes, key_scale, value_codes, value_scale, weight, ctx_len, start_shard, draft_depth)


def solution(mesh):
    torus = Mesh(
        mesh.devices.reshape(N, N, mesh.shape["head"], mesh.shape["req"]),
        ("seq_0", "seq_1", "head", "req"),
    )
    placed = (
        P("req", HEAD_SEQ, None),
        P("req", "head", SEQ, None),
        P("req", "head", SEQ),
        P("req", "head", SEQ, None),
        P("req", "head", SEQ),
        P("head", SEQ),
        P("req"),
        P("req"),
        P("req", None),
    )
    return jax.shard_map(
        on_device, mesh=torus, in_specs=placed, out_specs=P("head", "req", SEQ), check_vma=False
    )
```

time: 116 us -> 48 us (0.41)
  the two profiles are of different devices: /device:TPU:2 before, /device:TPU:8 now
where the time goes in v1:
time: 48 us; the launch traced here: 47.8 us
  Pallas kernels  46.6 us (97%)
  local copies, waits for them, and re-layouts  1.26 us (3%)
    pallas_call x1, Pallas kernels, on_device(): pl.pallas_call(kernel, out_shape=jax.ShapeDtypeStruct((1, R, width), b16)...  46.6 us
    unnamed x1, local copies, waits for them, and re-layouts  1.26 us

profile of v1, /device:TPU:8, one launch (start us, length us, event | category | flops | bytes accessed | tf_op | source)
XLA Modules:
  0.0 47.8 jit_solution(17151837573399925342)
XLA Ops:
  0.0 46.6 %draft_attention.1 = bf16[1,4,256]{2,1,0:T(4,128)(2,1)} custom-call(bf16[4,2,128]{2,1,0:T(2,128)(2,1)} %q_hbm.1, bf16[4,2,512,128]{3,2,1,0:T(8,128)(2,1)} %k_hbm.1, f32[4,2,8]{2,1,0:T(2,128)} %ks_hbm.1, bf16[4,2,512,128]{3,2,1,0:T(8,128)(2,1)} %v_hbm.1, f32[4,2,8]{2,1,0:T(2,128)} %vs_hbm.1, bf16[2,8,2,128,256]{4,3,2,1,0:T(8,128)(2,1)} %bitcast.1, s32[4]{0:T(128)} %ctx_hbm.1, ...), custom_call_target="tpu_custom_call" | custom-call | tf_op jit(solution)/shard_map/draft_attention/pallas_call | solution.py:292
  46.6 1.3 %copy.11 = bf16[1,4,256]{2,1,0:T(4,128)(2,1)} copy(bf16[1,4,256]{2,1,0:T(4,128)(2,1)} %draft_attention.1) | data formatting | bytes 4096

commit v2 on v1

v2 whole, which is shorter than its diff:
```python
import math

import jax
import jax.numpy as jnp
from jax import lax
from jax.experimental import pallas as pl
from jax.experimental.pallas import tpu as pltpu
from jax.sharding import Mesh
from jax.sharding import PartitionSpec as P

QHEADS = 128
KVH = 8
HD = 128
DRAFT = 4
BLK = 64
SEQ = ("seq_0", "seq_1")
HEAD_SEQ = ("head", "seq_0", "seq_1")
MESH = pl.DeviceIdType.MESH

N = 8
NX = 4
R = 4
KV = 2
ROWS = 64
KEYS = 512
NEG = -1e30
FLOOR = -1e29
ORDER = (4, 3, 5, 2, 6, 1, 7)
NEAR = ORDER[::-1]
FIRST = ("seq_1", "seq_0")
SECOND = ("seq_0", "seq_1")


def peer(axis, k, size):
    return lax.rem(lax.axis_index(axis) + k, size)


def f32(x):
    return x.astype(jnp.float32)


def bf16(x):
    return x.astype(jnp.bfloat16)


def kernel(
    q_hbm, k_hbm, ks_hbm, v_hbm, vs_hbm, w_hbm, ctx_hbm, start_hbm, depth_hbm,
    out_ref,
    q0, q1, qf, kbuf, vbuf, wbuf, ks, vs, ctx, start, depth,
    krow, vrow, bias, sacc, racc, cacc, dacc, att, ybuf,
    lsem, ssem, rsem, xs, xr,
):
    y = lax.axis_index("seq_0")
    z = lax.axis_index("seq_1")
    x = lax.axis_index("head")
    line = {"seq_0": y, "seq_1": z}
    here = y * N + z

    barrier = pltpu.get_barrier_semaphore()
    for axis in SEQ:
        for k in ORDER:
            pl.semaphore_signal(barrier, inc=1, device_id={axis: peer(axis, k, N)}, device_id_type=MESH)
    for k in (2, 1, 3):
        pl.semaphore_signal(barrier, inc=1, device_id={"head": peer("head", k, NX)}, device_id_type=MESH)

    qc0 = pltpu.make_async_copy(q_hbm.at[pl.ds(0, 2)], q0.at[:, z], lsem.at[0])
    qc1 = pltpu.make_async_copy(q_hbm.at[pl.ds(2, 2)], q1.at[:, y], lsem.at[1])
    qc0.start()
    qc1.start()
    small = [
        pltpu.make_async_copy(a, b, lsem.at[2 + i])
        for i, (a, b) in enumerate(
            ((ks_hbm, ks), (vs_hbm, vs), (ctx_hbm, ctx), (start_hbm, start), (depth_hbm, depth))
        )
    ]
    for c in small:
        c.start()
    kc = pltpu.make_async_copy(k_hbm, kbuf, lsem.at[7])
    vc = pltpu.make_async_copy(v_hbm, vbuf, lsem.at[8])
    wc = pltpu.make_async_copy(w_hbm, wbuf, lsem.at[9])
    kc.start()
    vc.start()
    wc.start()
    qc0.wait()
    qc1.wait()
    pl.semaphore_wait(barrier, 2 * (N - 1) + NX - 1)

    sent = []

    def send(src, dst, slot, axis, k):
        copy = pltpu.make_async_remote_copy(
            src_ref=src, dst_ref=dst, send_sem=ssem.at[slot, k - 1], recv_sem=rsem.at[slot, k - 1],
            device_id={axis: peer(axis, k, N)}, device_id_type=MESH,
        )
        copy.start()
        sent.append(copy)

    def arrived(src, dst, slot, axis, k):
        pltpu.make_async_remote_copy(
            src_ref=src, dst_ref=dst, send_sem=ssem.at[slot, k - 1], recv_sem=rsem.at[slot, k - 1],
            device_id={axis: peer(axis, k, N)}, device_id_type=MESH,
        ).wait_recv()

    for k in ORDER:
        send(q0.at[:, z], q0.at[:, z], 0, "seq_1", k)
        send(q1.at[:, y], q1.at[:, y], 1, "seq_0", k)

    for c in small:
        c.wait()
    lane_row = lax.broadcasted_iota(jnp.int32, (1, HD), 1)
    lane_key = lax.broadcasted_iota(jnp.int32, (8, KEYS), 1)
    draft = lax.rem(lax.broadcasted_iota(jnp.int32, (8, KEYS), 0), DRAFT)
    factor = math.log2(math.e) / math.sqrt(HD)
    for r in range(R):
        offset = lax.rem(here - start[r] + N * N, N * N) * KEYS
        base = ctx[r] - DRAFT - offset
        limit = jnp.full((8, KEYS), base + depth[r, 0], jnp.int32)
        for t in range(1, DRAFT):
            limit = jnp.where(draft == t, base + depth[r, t], limit)
        bias[r] = jnp.where(lane_key <= limit, 0.0, NEG)
        for h in range(KV):
            for j in range(KEYS // HD):
                cols = pl.ds(j * HD, HD)
                krow[r, h, :, cols] = jnp.where(lane_row < BLK, ks[r, h, 2 * j], ks[r, h, 2 * j + 1]) * factor
                vrow[r, h, :, cols] = jnp.where(lane_row < BLK, vs[r, h, 2 * j], vs[r, h, 2 * j + 1])

    for k in NEAR:
        arrived(q1.at[:, y], q1.at[:, peer("seq_0", N - k, N)], 1, "seq_0", k)
    for k in ORDER:
        send(q1, qf.at[pl.ds(2, 2), :, z], 3, "seq_1", k)
    for k in NEAR:
        arrived(q0.at[:, z], q0.at[:, peer("seq_1", N - k, N)], 0, "seq_1", k)
    for k in ORDER:
        send(q0, qf.at[pl.ds(0, 2), y], 2, "seq_0", k)
    qf[0:2, y] = q0[...]
    qf[2:4, :, z] = q1[...]

    lane8 = lax.broadcasted_iota(jnp.int32, (8, HD), 1)
    row8 = lax.broadcasted_iota(jnp.int32, (8, HD), 0)
    own_lane = lax.rem(lane8, 8) == row8

    def split_rows(v):
        high = f32(bf16(v))
        rest = v - high
        mid = f32(bf16(rest))
        rows = jnp.where(row8[None] == 0, high, jnp.where(row8[None] == 1, mid, rest - mid))
        return bf16(jnp.where(row8[None] < 3, rows, 0.0))

    pick = [jnp.logical_and(own_lane, lax.div(lane8, 8) == q) for q in range(8)]

    kc.wait()
    vc.wait()
    for half in range(2):
        for k in NEAR:
            if half == 0:
                arrived(q0, qf.at[pl.ds(0, 2), peer("seq_0", N - k, N)], 2, "seq_0", k)
            else:
                arrived(q1, qf.at[pl.ds(2, 2), :, peer("seq_1", N - k, N)], 3, "seq_1", k)
        axis = FIRST[half]
        stats = jnp.zeros((N, 8, HD), jnp.float32)
        accs = {}
        for r2 in range(2):
            r = half * 2 + r2
            for h in range(KV):
                rows = qf[r, 4 * h : 4 * h + 4].reshape(ROWS, HD)
                raw = lax.dot_general(
                    rows, kbuf[r, h], (((1,), (1,)), ((), ())), preferred_element_type=jnp.float32
                )
                score = (raw * krow[r, h]).reshape(N, 8, KEYS) + bias[r][None]
                top = jnp.maximum(jnp.max(score, axis=2, keepdims=True), FLOOR)
                weight = jnp.exp2(score - top)
                total = jnp.sum(weight, axis=2, keepdims=True)
                scaled = bf16(weight.reshape(ROWS, KEYS) * vrow[r, h])
                accs[r2, h] = jnp.dot(scaled, vbuf[r, h], preferred_element_type=jnp.float32)
                c = r2 * KV + h
                stats = jnp.where(pick[c][None], top, stats)
                stats = jnp.where(pick[4 + c][None], total, stats)
        sacc[half, :, 32:40] = split_rows(jnp.sum(stats, axis=1, keepdims=True))
        for o in range(N):
            for h in range(KV):
                part = jnp.concatenate([accs[r2, h][8 * o : 8 * o + 8] for r2 in range(2)], axis=0)
                sacc[half, o, 16 * h : 16 * h + 16] = bf16(part)
        me = line[axis]
        for k in ORDER:
            send(sacc.at[half, peer(axis, k, N)], racc.at[half, me], 4 + half, axis, k)
        racc[half, me] = sacc[half, me]

    low = lane_row < 4 * 8

    def combine(accs, half, last):
        st = jnp.sum(f32(accs[half, :, 32:40]), axis=1)
        top = jnp.max(st, axis=0, keepdims=True)
        f = jnp.exp2(st - top)
        total = jnp.sum(f * pltpu.roll(st, HD - 32, 1), axis=0, keepdims=True)
        if last:
            f = f * jnp.where(low, 1.0 / total, 0.0)
        outs = [jnp.zeros((16, HD), jnp.float32) for h in range(KV)]
        for k in range(N):
            row = jnp.broadcast_to(f[k : k + 1], (8, HD))
            cols = [jnp.sum(jnp.where(pick[c], row, 0.0), axis=1, keepdims=True) for c in range(4)]
            for h in range(KV):
                w = jnp.concatenate([jnp.broadcast_to(cols[r2 * KV + h], (8, HD)) for r2 in range(2)], axis=0)
                outs[h] = outs[h] + f32(accs[half, k, 16 * h : 16 * h + 16]) * w
        return [bf16(o) for o in outs], jnp.where(low, top, pltpu.roll(total, 32, 1))

    for half in (1, 0):
        axis = FIRST[half]
        for k in NEAR:
            arrived(sacc.at[half, 0], racc.at[half, peer(axis, N - k, N)], 4 + half, axis, k)
        outs, st = combine(racc, half, False)
        for h in range(KV):
            cacc[half, 16 * h : 16 * h + 16] = outs[h]
        cacc[half, 32:40] = split_rows(st[None])[0]
        axis = SECOND[half]
        me = line[axis]
        for k in ORDER:
            send(cacc.at[half], dacc.at[half, me], 6 + half, axis, k)
        dacc[half, me] = cacc[half]

    for half in range(2):
        axis = SECOND[half]
        for k in NEAR:
            arrived(cacc.at[half], dacc.at[half, peer(axis, N - k, N)], 6 + half, axis, k)
        outs, _ = combine(dacc, half, True)
        axis = FIRST[half]
        me = line[axis]
        for h in range(KV):
            att[me, half, h] = outs[h]
        for k in ORDER:
            send(att.at[me, half], att.at[me, half], 8 + half, axis, k)

    wc.wait()
    width = wbuf.shape[-1]
    prods = [[None, None], [None, None]]

    def project(half, o):
        lhs = jnp.concatenate([att[o, half, h] for h in range(KV)], axis=1)
        for jj in range(2):
            w = jnp.concatenate([wbuf[h, o, jj] for h in range(KV)], axis=0)
            p = jnp.dot(lhs, w, preferred_element_type=jnp.float32)
            prods[half][jj] = p if prods[half][jj] is None else prods[half][jj] + p

    for half in range(2):
        project(half, line[FIRST[half]])
    for k in NEAR:
        for half in (1, 0):
            axis = FIRST[half]
            frm = peer(axis, N - k, N)
            arrived(att.at[line[axis], half], att.at[frm, half], 8 + half, axis, k)
            project(half, frm)
    sub = lax.rem(lax.broadcasted_iota(jnp.int32, (16, width), 0), 8)
    for half in range(2):
        both = jnp.where(sub < 4, prods[half][0], prods[half][1])
        for r2 in range(2):
            b = 8 * r2
            ybuf[:, 2 * half + r2, :] = both[b : b + 4] + both[b + 4 : b + 8]

    xcopies = []
    for k in (2, 1, 3):
        to = peer("head", k, NX)
        copy = pltpu.make_async_remote_copy(
            src_ref=ybuf.at[to], dst_ref=out_ref.at[x], send_sem=xs.at[k - 1], recv_sem=xr.at[k - 1],
            device_id={"head": to}, device_id_type=MESH,
        )
        copy.start()
        xcopies.append((k, copy))
    mine = pltpu.make_async_copy(ybuf.at[x], out_ref.at[x], lsem.at[0])
    mine.start()
    for c in sent:
        c.wait_send()
    mine.wait()
    for k, copy in xcopies[::-1]:
        frm = peer("head", NX - k, NX)
        pltpu.make_async_remote_copy(
            src_ref=ybuf.at[0], dst_ref=out_ref.at[frm], send_sem=xs.at[k - 1], recv_sem=xr.at[k - 1],
            device_id={"head": frm}, device_id_type=MESH,
        ).wait_recv()
    for k, copy in xcopies:
        copy.wait_send()


def on_device(queries, key_codes, key_scale, value_codes, value_scale, out_weight, ctx_len, start_shard, draft_depth):
    width = out_weight.shape[1]
    weight = out_weight.reshape(KV, N, 2, HD, width)
    dma = pltpu.SemaphoreType.DMA
    b16, flt, i32 = jnp.bfloat16, jnp.float32, jnp.int32
    vm, sm = pltpu.VMEM, pltpu.SMEM
    shares = pl.pallas_call(
        kernel,
        out_shape=jax.ShapeDtypeStruct((NX, R, width), flt),
        in_specs=[pl.BlockSpec(memory_space=pltpu.HBM)] * 9,
        out_specs=pl.BlockSpec(memory_space=pltpu.HBM),
        scratch_shapes=[
            vm((2, N, 2, HD), b16),
            vm((2, N, 2, HD), b16),
            vm((R, N, N, 2, HD), b16),
            vm((R, KV, KEYS, HD), b16),
            vm((R, KV, KEYS, HD), b16),
            vm((KV, N, 2, HD, width), b16),
            sm((R, KV, KEYS // BLK), flt),
            sm((R, KV, KEYS // BLK), flt),
            sm((R,), i32),
            sm((R,), i32),
            sm((R, DRAFT), i32),
            vm((R, KV, 1, KEYS), flt),
            vm((R, KV, 1, KEYS), flt),
            vm((R, 8, KEYS), flt),
            vm((2, N, 40, HD), b16),
            vm((2, N, 40, HD), b16),
            vm((2, 40, HD), b16),
            vm((2, N, 40, HD), b16),
            vm((N, 2, KV, 16, HD), b16),
            vm((DRAFT, R, width), flt),
            dma((10,)),
            dma((10, N - 1)),
            dma((10, N - 1)),
            dma((NX - 1,)),
            dma((NX - 1,)),
        ],
        compiler_params=pltpu.CompilerParams(collective_id=0, has_side_effects=True),
        name="draft_attention",
    )(queries, key_codes, key_scale, value_codes, value_scale, weight, ctx_len, start_shard, draft_depth)
    return bf16(jnp.sum(shares, axis=0, keepdims=True))


def solution(mesh):
    torus = Mesh(
        mesh.devices.reshape(N, N, mesh.shape["head"], mesh.shape["req"]),
        ("seq_0", "seq_1", "head", "req"),
    )
    placed = (
        P("req", HEAD_SEQ, None),
        P("req", "head", SEQ, None),
        P("req", "head", SEQ),
        P("req", "head", SEQ, None),
        P("req", "head", SEQ),
        P("head", SEQ),
        P("req"),
        P("req"),
        P("req", None),
    )
    return jax.shard_map(
        on_device, mesh=torus, in_specs=placed, out_specs=P("head", "req", SEQ), check_vma=False
    )
```

time: 48 us -> 47 us (0.979)
  other arithmetic: 0 us -> 1.31 us
  local copies, waits for them, and re-layouts: 1.26 us -> 0 us
  Pallas kernels: 46.6 us -> 45.5 us
    reduce_sum x0 -> x1, other arithmetic: none -> 1.31 us  [on_device(): return bf16(jnp.sum(shares, axis=0, keepdims=True))]
    unnamed x1 -> x0, local copies, waits for them, and re-layouts: 1.26 us -> none
    pallas_call x1, Pallas kernels: 46.6 us -> 45.5 us  [on_device(): pl.pallas_call(kernel, out_shape=jax.ShapeDtypeStruct((NX, R, width), flt...]
where the time goes in v2:
time: 47 us; the launch traced here: 46.8 us
  Pallas kernels  45.5 us (97%)
  other arithmetic  1.31 us (3%)
    pallas_call x1, Pallas kernels, on_device(): pl.pallas_call(kernel, out_shape=jax.ShapeDtypeStruct((NX, R, width), flt...  45.5 us
    reduce_sum x1, other arithmetic, on_device(): return bf16(jnp.sum(shares, axis=0, keepdims=True))  1.31 us

profile of v2, /device:TPU:8, one launch (start us, length us, event | category | flops | bytes accessed | tf_op | source)
XLA Modules:
  0.0 46.8 jit_solution(18152998313592294208)
XLA Ops:
  0.0 45.5 %draft_attention.1 = f32[4,4,256]{2,1,0:T(4,128)} custom-call(bf16[4,2,128]{2,1,0:T(2,128)(2,1)} %q_hbm.1, bf16[4,2,512,128]{3,2,1,0:T(8,128)(2,1)} %k_hbm.1, f32[4,2,8]{2,1,0:T(2,128)} %ks_hbm.1, bf16[4,2,512,128]{3,2,1,0:T(8,128)(2,1)} %v_hbm.1, f32[4,2,8]{2,1,0:T(2,128)} %vs_hbm.1, bf16[2,8,2,128,256]{4,3,2,1,0:T(8,128)(2,1)} %bitcast.4, s32[4]{0:T(128)} %ctx_hbm.1, ...), custom_call_target="tpu_custom_call" | custom-call | tf_op jit(solution)/shard_map/draft_attention/pallas_call | solution.py:288
  45.5 1.3 %reduce_sum.9 = bf16[4,256]{1,0:T(4,128)(2,1)} reduce(f32[4,4,256]{2,1,0:T(4,128)} %draft_attention.1, f32[]{:T(128)} %constant.0.clone.1), dimensions={0}, to_apply=%region_0.0 | reduce | flops 3072 | bytes 18436 | tf_op jit(solution)/shard_map/reduce_sum | solution.py:323
